TPU v7x, 32 devices: a whole 2x2x4 slice. The times are simulated.
32 devices in a mesh: feat: 4 (over y, core), dom: 8 (over z, x).
Axes of the slice: x: 2, y: 2, z: 4, core: 2. Of those that a mesh axis runs over, the one named last changes fastest.
Arguments:
- features: bfloat16 [32768, 128], P('dom'), may hold values from -6 to 6
- w_input: bfloat16 [128, 256], P(None, 'feat'), may hold values from -0.5 to 0.5
- layer_weights: bfloat16 [4, 256, 256], replicated, may hold values from -0.375 to 0.375
- history: bfloat16 [4, 32768, 256], P(None, 'dom', 'feat'), may hold values from 0 to 2
- tile_values: bfloat16 [256, 6, 128, 128], P('dom'), may hold values from -0.21875 to 0.21875
- tile_columns: int32 [256, 6], P('dom'), may hold values from 0 to 63, as said below
- send_rows: int32 [8, 8, 512], P('dom'), may hold values from 0 to 4095
- send_counts: int32 [8, 8], P('dom'), may hold values from 0 to 512, as said below
Outputs:
- pushed: bfloat16 [4, 32768, 256], P(None, 'dom', 'feat')
- final_rows: bfloat16 [32768, 256], P('dom', 'feat')
Inputs may be any that keep to these rules, and one draw needn't show every extreme that they name: `tile_columns`: per row of tiles the first 2 entries lie below 4096 / 128 (own rows), the others at or above it (halo slots); every halo column tile of every partition is named somewhere. `send_counts`: A partition sends nothing to itself; in every draw some destination receives exactly 512 rows from every other partition.
All inputs are finite; a program needn't handle non-finite values.
Results may differ from a plain program's by a relative error of at most 0.0052.
Values may be sent and summed in bfloat16 or wider, within the bound.
A program may use at most 128 MiB of HBM per device.

v0:
```python
import functools
import math

import jax
import jax.numpy as jnp
from jax import lax
from jax.experimental import pallas as pl
from jax.experimental.pallas import tpu as pltpu
from jax.sharding import PartitionSpec as P

ALPHA = 0.1
LAMBDA_DECAY = 0.5
CORES = 2
OWN_TILES = 2
LAG = 2
MESH = pl.DeviceIdType.MESH
NT = (((1,), (1,)), ((), ()))


def kernel(
    doms, feats, layers, tile, columns_ref, counts_ref, rows_ref, history_hbm, features_hbm,
    w_ref, weights_ref, values_hbm, pushed_hbm, final_hbm, *scratch
):
    halos = scratch[:layers]
    (history, features, w_all, weights_t, values, outgoing, initial, ping, pong,
     load_sem, w_send, w_recv, z_send, z_recv, y_send, y_recv, c_send, c_recv, out_sem) = scratch[layers:]
    width = w_ref.shape[0]
    nodes = history.shape[1]
    cap = rows_ref.shape[1]
    row_tiles, per_row = values.shape[0], values.shape[1]
    chips = feats // CORES
    dom = lax.axis_index("dom")
    feat = lax.axis_index("feat")
    chip, core = feat // CORES, feat % CORES
    sibling = chip * CORES + (1 - core)

    loads = [
        pltpu.make_async_copy(history_hbm, history, load_sem.at[0]),
        pltpu.make_async_copy(features_hbm, features, load_sem.at[1]),
        pltpu.make_async_copy(values_hbm, values, load_sem.at[2]),
    ]
    for load in loads:
        load.start()

    barrier = pltpu.get_barrier_semaphore()
    for step in range(1, doms):
        pl.semaphore_signal(
            barrier, inc=1, device_id={"dom": lax.rem(dom + step, doms)}, device_id_type=MESH
        )
    for step in range(1, feats):
        pl.semaphore_signal(
            barrier, inc=1, device_id={"feat": lax.rem(feat + step, feats)}, device_id_type=MESH
        )

    def slice_rows(index):
        return pl.ds(pl.multiple_of(index * width, width), width)

    blocks = cap // tile

    def partner(step):
        flips, bit = lax.rem(step, 2) * (doms // 2) + step // 2, 1
        dest = dom
        while bit < doms:
            dest = dest + lax.rem(flips // bit, 2) * (bit - 2 * bit * lax.rem(dom // bit, 2))
            bit *= 2
        return dest

    def block_tiles(source):
        return pl.ds(source * blocks, blocks)

    def w_copy(step):
        return pltpu.make_async_remote_copy(
            src_ref=w_ref,
            dst_ref=w_all.at[slice_rows(feat)],
            send_sem=w_send.at[step],
            recv_sem=w_recv.at[step],
            device_id={"feat": lax.rem(feat + step, feats)},
            device_id_type=MESH,
        )

    def z_copy(level, step):
        dest = partner(step)
        return pltpu.make_async_remote_copy(
            src_ref=outgoing.at[step, :, pl.ds(level * width, width)],
            dst_ref=halos[level].at[block_tiles(dom), slice_rows(feat)],
            send_sem=z_send.at[level, step],
            recv_sem=z_recv.at[level, step],
            device_id={"dom": dest},
            device_id_type=MESH,
        )

    def y_copy(level, step, hop):
        source = partner(step)
        block = halos[level].at[block_tiles(source), slice_rows(feat)]
        return pltpu.make_async_remote_copy(
            src_ref=block,
            dst_ref=block,
            send_sem=y_send.at[level, step, hop],
            recv_sem=y_recv.at[level, step, hop],
            device_id={"feat": lax.rem(chip + hop, chips) * CORES + core},
            device_id_type=MESH,
        )

    def c_copy(level, step, hop):
        source = partner(step)
        owner = lax.rem(chip + chips - hop, chips) * CORES + core
        block = halos[level].at[block_tiles(source), slice_rows(owner)]
        return pltpu.make_async_remote_copy(
            src_ref=block,
            dst_ref=block,
            send_sem=c_send.at[level, step, hop],
            recv_sem=c_recv.at[level, step, hop],
            device_id={"feat": sibling},
            device_id_type=MESH,
        )

    def gather(step):
        dest = partner(step)
        part = min(cap, 256)
        for begin in range(0, cap, part):
            slots = begin + lax.broadcasted_iota(jnp.int32, (1, part), 1)
            rows = rows_ref[pl.ds(dest, 1), pl.ds(begin, part)]
            rows = jnp.where(slots < counts_ref[0, dest], rows, -1)
            nodes_iota = lax.broadcasted_iota(jnp.int32, (nodes, part), 0)
            onehot = jnp.where(nodes_iota == rows, 1.0, 0.0).astype(jnp.bfloat16)
            picked = jnp.dot(history[...], onehot, preferred_element_type=jnp.float32)
            picked = picked.astype(jnp.bfloat16)
            for offset in range(0, part, tile):
                outgoing[step, (begin + offset) // tile] = picked[:, offset : offset + tile]

    loads[0].wait()
    gather(1)
    pl.semaphore_wait(barrier, doms + feats - 2)
    for step in range(1, feats):
        w_copy(step).start()
    z_copy(0, 1).start()

    def gather_step(step, carry):
        gather(step)
        z_copy(0, step).start()
        return carry

    lax.fori_loop(2, doms, gather_step, 0)
    for level in range(layers):
        halos[level][block_tiles(dom)] = jnp.zeros((blocks, width * feats, tile), jnp.bfloat16)
        weights_t[level] = weights_ref[level].astype(jnp.float32).T.astype(jnp.bfloat16)

    w_all[slice_rows(feat), :] = w_ref[...]
    for step in range(1, feats):
        w_copy(step).wait_recv()
    loads[1].wait()
    group = row_tiles // doms

    def initial_group(index):
        span = group * tile
        part = pl.ds(pl.multiple_of(index * span, span), span)
        product = lax.dot_general(
            w_all[...], features[part, :], NT, preferred_element_type=jnp.float32
        )
        product = jnp.maximum(product, 0.0).astype(jnp.bfloat16)
        for offset in range(group):
            initial[index * group + offset] = product[:, offset * tile : (offset + 1) * tile]

    def push(level, buffer):
        target = pushed_hbm.at[level] if level < layers else final_hbm
        return pltpu.make_async_copy(buffer.at[:, slice_rows(feat)], target, out_sem.at[level])

    states = [initial] + [ping if index % 2 == 0 else pong for index in range(layers)]

    def layer_group(layer, index):
        beta = math.log(LAMBDA_DECAY / (layer + 1) + 1.0)
        current, following, halo = states[layer], states[layer + 1], halos[layer]
        pieces = []
        for offset in range(group):
            row = index * group + offset
            picked = []
            for k in range(per_row):
                column = columns_ref[k, row]
                if k < OWN_TILES:
                    picked.append(current[column])
                else:
                    picked.append(halo[jnp.maximum(column - row_tiles, 0)])
            total = lax.dot_general(
                jnp.concatenate(picked, axis=1),
                jnp.concatenate([values[row, k] for k in range(per_row)], axis=1),
                NT,
                preferred_element_type=jnp.float32,
            )
            pieces.append(total)
        first = index * group
        start = jnp.concatenate([initial[first + offset] for offset in range(group)], axis=1)
        aggregated = jnp.concatenate(pieces, axis=1) if group > 1 else pieces[0]
        blended = (
            (1.0 - ALPHA) * aggregated + ALPHA * start.astype(jnp.float32)
        ).astype(jnp.bfloat16)
        product = jnp.dot(weights_t[layer], blended, preferred_element_type=jnp.float32)
        fresh = jnp.maximum((1.0 - beta) * blended.astype(jnp.float32) + beta * product, 0.0)
        fresh = fresh.astype(jnp.bfloat16)
        for offset in range(group):
            following[first + offset] = fresh[:, offset * tile : (offset + 1) * tile]

    def arrive(level, step):
        z_copy(level, step).wait_recv()
        if level + 1 < layers:
            z_copy(level + 1, step).start()
        for hop in range(1, chips):
            y_copy(level, step, hop).start()
        c_copy(level, step, 0).start()

    def relay(level, step):
        for hop in range(1, chips):
            y_copy(level, step, hop).wait_recv()
            c_copy(level, step, hop).start()

    for level in range(layers + 1):
        if level >= 3:
            push(level - 2, states[level - 2]).wait()

        def early(step, carry, level=level):
            if level < layers:
                arrive(level, step)
            if level >= 1:
                relay(level - 1, step + doms - 1 - LAG)
            else:
                initial_group(step)
            if level >= 2:
                layer_group(level - 2, step + doms - 2 - LAG)
            return carry

        lax.fori_loop(1, 1 + LAG, early, 0)
        if level >= 2:
            layer_group(level - 2, doms - 1)
            push(level - 1, states[level - 1]).start()
        if level >= 1:

            def settle(step, carry, level=level):
                for hop in range(chips):
                    c_copy(level - 1, step, hop).wait_recv()
                return carry

            lax.fori_loop(1, doms, settle, 0)
        else:
            initial_group(0)
        if level == 1:
            loads[2].wait()

        def late(step, carry, level=level):
            if level < layers:
                arrive(level, step)
                relay(level, step - LAG)
            if level == 0:
                initial_group(step)
            elif level < layers:
                layer_group(level - 1, step - 1 - LAG)
            return carry

        if level < layers:
            lax.fori_loop(1 + LAG, doms, late, 0)
        if level == 0:
            push(0, initial).start()

    def last_step(index, carry):
        layer_group(layers - 1, index)
        return carry

    lax.fori_loop(0, doms, last_step, 0)
    push(layers, states[layers]).start()

    for step in range(1, feats):
        w_copy(step).wait_send()
    for level in range(layers):

        def drain(step, carry, level=level):
            z_copy(level, step).wait_send()
            for hop in range(chips):
                c_copy(level, step, hop).wait_send()
            for hop in range(1, chips):
                y_copy(level, step, hop).wait_send()
            return carry

        lax.fori_loop(1, doms, drain, 0)
    waited = set(range(1, layers - 1))
    for level in range(layers + 1):
        if level not in waited:
            push(level, states[level]).wait()


def on_device(doms, feats, features, w_input, layer_weights, history, tile_values, tile_columns, send_rows, send_counts):
    layers, nodes, width = history.shape
    row_tiles, per_row, tile, _ = tile_values.shape
    cap = send_rows.shape[2]
    hidden = width * feats
    chips = feats // CORES
    any_spec = pl.BlockSpec(memory_space=pl.ANY)
    vmem = pl.BlockSpec(memory_space=pltpu.VMEM)
    smem = pl.BlockSpec(memory_space=pltpu.SMEM)
    bf16 = jnp.bfloat16
    dma = pltpu.SemaphoreType.DMA
    pushed, final = pl.pallas_call(
        functools.partial(kernel, doms, feats, layers, tile),
        out_shape=(
            jax.ShapeDtypeStruct((layers, row_tiles, width, tile), bf16),
            jax.ShapeDtypeStruct((row_tiles, width, tile), bf16),
        ),
        in_specs=[smem, smem, vmem, any_spec, any_spec, vmem, vmem, any_spec],
        out_specs=(any_spec, any_spec),
        scratch_shapes=[pltpu.VMEM((doms * cap // tile, hidden, tile), bf16) for _ in range(layers)] + [
            pltpu.VMEM((layers * width, nodes), bf16),
            pltpu.VMEM(features.shape, bf16),
            pltpu.VMEM((hidden, features.shape[1]), bf16),
            pltpu.VMEM((layers, hidden, hidden), bf16),
            pltpu.VMEM(tile_values.shape, bf16),
            pltpu.VMEM((doms, cap // tile, layers * width, tile), bf16),
            pltpu.VMEM((row_tiles, hidden, tile), bf16),
            pltpu.VMEM((row_tiles, hidden, tile), bf16),
            pltpu.VMEM((row_tiles, hidden, tile), bf16),
            dma((3,)),
            dma((feats,)),
            dma((feats,)),
            dma((layers, doms)),
            dma((layers, doms)),
            dma((layers, doms, chips)),
            dma((layers, doms, chips)),
            dma((layers, doms, chips)),
            dma((layers, doms, chips)),
            dma((layers + 1,)),
        ],
        compiler_params=pltpu.CompilerParams(
            collective_id=0, has_side_effects=True, vmem_limit_bytes=67043328
        ),
    )(
        tile_columns.T,
        send_counts,
        send_rows[0],
        jnp.swapaxes(history, 1, 2).reshape(layers * width, nodes),
        features,
        w_input.T,
        layer_weights,
        tile_values,
    )
    pushed = jnp.transpose(pushed, (0, 1, 3, 2)).reshape(layers, nodes, width)
    return pushed, jnp.transpose(final, (0, 2, 1)).reshape(nodes, width)


def solution(mesh):
    placed = (
        P("dom", None),
        P(None, "feat"),
        P(),
        P(None, "dom", "feat"),
        P("dom", None, None, None),
        P("dom", None),
        P("dom", None, None),
        P("dom", None),
    )
    return jax.shard_map(
        functools.partial(on_device, mesh.shape["dom"], mesh.shape["feat"]),
        mesh=mesh,
        in_specs=placed,
        out_specs=(P(None, "dom", "feat"), P("dom", "feat")),
        check_vma=False,
    )
```

profile of v0, /device:TPU:0, one launch (start us, length us, event | category | flops | bytes accessed | tf_op | source)
XLA Modules:
  0.0 79.6 jit_solution(7478473599669503881)
XLA Ops:
  0.6 74.8 %shard_map.95 = (bf16[4,32,64,128]{3,2,1,0:T(8,128)(2,1)}, bf16[32,64,128]{2,1,0:T(8,128)(2,1)}) custom-call(s32[6,32]{1,0:T(8,128)} %bitcast.21, s32[1,8]{1,0:T(1,128)} %counts_ref.1, s32[8,512]{1,0:T(8,128)} %bitcast.19, bf16[256,4096]{1,0:T(8,128)(2,1)} %bitcast.18, bf16[4096,128]{1,0:T(8,128)(2,1)} %features_hbm.1, bf16[64,128]{1,0:T(8,128)(2,1)} %bitcast.20, ...), custom_call_target="tpu_custom_call" | custom-call | tf_op jit(solution)/shard_map/pallas_call | solution.py:299
  75.5 0.0 copy-start
  75.5 3.3 %copy_bitcast_fusion = bf16[4,4096,64]{1,2,0:T(8,128)(2,1)} fusion(bf16[4,32,64,128]{3,2,1,0:T(8,128)(2,1)} %get-tuple-element.4), kind=kLoop, calls=%fused_computation | loop fusion | bytes 4194304 | tf_op jit(solution)/shard_map/reshape | solution.py:341
  78.8 0.0 copy-done
  78.8 0.9 %copy_bitcast_fusion.1 = bf16[4096,64]{0,1:T(8,128)(2,1)} fusion(bf16[32,64,128]{2,1,0:T(8,128)(2,1)S(1)} %copy-done), kind=kLoop, calls=%fused_computation.1 | loop fusion | bytes 1048576 | tf_op jit(solution)/shard_map/reshape | solution.py:342
Async XLA Ops:
  75.5 3.3 %copy-start = (bf16[32,64,128]{2,1,0:T(8,128)(2,1)S(1)}, bf16[32,64,128]{2,1,0:T(8,128)(2,1)}, u32[]{:S(2)}) copy-start(bf16[32,64,128]{2,1,0:T(8,128)(2,1)} %get-tuple-element.5) | copy-start | bytes 1572868
where the time goes:
time: 79.8 us; the launch traced here: 79.6 us
  Pallas kernels  74.8 us (94%)
  local copies, waits for them, and re-layouts  4.16 us (5%)
    pallas_call x1, Pallas kernels, on_device(): pl.pallas_call(functools.partial(kernel, doms, feats, layers, tile), out_...  74.8 us
    reshape x1, local copies, waits for them, and re-layouts, on_device(): pushed = jnp.transpose(pushed, (0, 1, 3, 2)).reshape(layers, nodes, width)  3.29 us

commit v1 on v0

v1 whole, which is shorter than its diff:
```python
import functools
import math

import jax
import jax.numpy as jnp
from jax import lax
from jax.experimental import pallas as pl
from jax.experimental.pallas import tpu as pltpu
from jax.sharding import PartitionSpec as P

ALPHA = 0.1
LAMBDA_DECAY = 0.5
CORES = 2
GROUP = 4
GATHER_LAG = 3
OWN_TILES = 2
MESH = pl.DeviceIdType.MESH
NT = (((1,), (1,)), ((), ()))


def gather_order(doms):
    quarter = doms // 4
    places = []
    for place in range(quarter):
        places.append(("I", place))
        places += [("N", index) for index in (2 * place, 2 * place + 1) if index < doms // 2 - 1]
        places.append(("O", place))
    return places


def kernel(
    doms, feats, layers, tile, columns_ref, counts_ref, rows_ref, history_hbm, features_hbm,
    w_ref, weights_ref, values_hbm, pushed_hbm, final_hbm, *scratch
):
    halos = scratch[:layers]
    (history, features, w_all, weights_t, last_w, values, outgoing, initial, ping, pong, partial, final,
     load_sem, w_send, w_recv, z_send, z_recv, y_send, y_recv, c_send, c_recv, out_sem,
     final_sem) = scratch[layers:]
    width = w_ref.shape[0]
    nodes = history.shape[1]
    cap = rows_ref.shape[1]
    row_tiles, per_row = values.shape[0], values.shape[1]
    hidden = width * feats
    chips = feats // CORES
    dom = lax.axis_index("dom")
    feat = lax.axis_index("feat")
    chip, core = feat // CORES, feat % CORES
    sibling = chip * CORES + (1 - core)

    loads = [
        pltpu.make_async_copy(history_hbm, history, load_sem.at[0]),
        pltpu.make_async_copy(features_hbm, features, load_sem.at[1]),
        pltpu.make_async_copy(values_hbm, values, load_sem.at[2]),
    ]
    for load in loads:
        load.start()

    barrier = pltpu.get_barrier_semaphore()
    for step in range(1, doms):
        pl.semaphore_signal(
            barrier, inc=1, device_id={"dom": lax.rem(dom + step, doms)}, device_id_type=MESH
        )
    for step in range(1, feats):
        pl.semaphore_signal(
            barrier, inc=1, device_id={"feat": lax.rem(feat + step, feats)}, device_id_type=MESH
        )

    def slice_rows(index):
        return pl.ds(pl.multiple_of(index * width, width), width)

    blocks = cap // tile

    half, quarter = doms // 2, doms // 4
    inside = lax.rem(dom // quarter + 1, 4) // 2
    near = [(flips, 0) for flips in range(1, half)]
    outer = [(half + quarter + index, -quarter) for index in range(quarter)]
    inner = [(half + index, quarter) for index in range(quarter)]
    groups = {"N": near, "O": outer, "I": inner}

    def chosen(table, index):
        if isinstance(index, int):
            base, slope = table[index]
            return base + slope * inside
        value = 0
        for place, (base, slope) in enumerate(table):
            value = value + jnp.where(index == place, base + slope * inside, 0)
        return value

    def partner(flips):
        dest, bit = dom, 1
        while bit < doms:
            dest = dest + lax.rem(flips // bit, 2) * (bit - 2 * bit * lax.rem(dom // bit, 2))
            bit *= 2
        return dest

    def block_tiles(source):
        return pl.ds(source * blocks, blocks)

    def w_copy(step):
        return pltpu.make_async_remote_copy(
            src_ref=w_ref,
            dst_ref=w_all.at[slice_rows(feat)],
            send_sem=w_send.at[step],
            recv_sem=w_recv.at[step],
            device_id={"feat": lax.rem(feat + step, feats)},
            device_id_type=MESH,
        )

    def z_copy(level, flips):
        return pltpu.make_async_remote_copy(
            src_ref=outgoing.at[flips, :, pl.ds(level * width, width)],
            dst_ref=halos[level].at[block_tiles(dom), slice_rows(feat)],
            send_sem=z_send.at[level, flips],
            recv_sem=z_recv.at[level, flips],
            device_id={"dom": partner(flips)},
            device_id_type=MESH,
        )

    def y_copy(level, flips, hop):
        block = halos[level].at[block_tiles(partner(flips)), slice_rows(feat)]
        return pltpu.make_async_remote_copy(
            src_ref=block,
            dst_ref=block,
            send_sem=y_send.at[level, flips, hop],
            recv_sem=y_recv.at[level, flips, hop],
            device_id={"feat": lax.rem(chip + hop, chips) * CORES + core},
            device_id_type=MESH,
        )

    def c_copy(level, flips, hop):
        owner = lax.rem(chip + chips - hop, chips) * CORES + core
        block = halos[level].at[block_tiles(partner(flips)), slice_rows(owner)]
        return pltpu.make_async_remote_copy(
            src_ref=block,
            dst_ref=block,
            send_sem=c_send.at[level, flips, hop],
            recv_sem=c_recv.at[level, flips, hop],
            device_id={"feat": sibling},
            device_id_type=MESH,
        )

    def gather(flips):
        dest = partner(flips)
        part = min(cap, 256)
        for begin in range(0, cap, part):
            slots = begin + lax.broadcasted_iota(jnp.int32, (1, part), 1)
            rows = rows_ref[pl.ds(dest, 1), pl.ds(begin, part)]
            rows = jnp.where(slots < counts_ref[0, dest], rows, -1)
            nodes_iota = lax.broadcasted_iota(jnp.int32, (nodes, part), 0)
            onehot = jnp.where(nodes_iota == rows, 1.0, 0.0).astype(jnp.bfloat16)
            picked = jnp.dot(history[...], onehot, preferred_element_type=jnp.float32)
            picked = picked.astype(jnp.bfloat16)
            for offset in range(0, part, tile):
                outgoing[flips, (begin + offset) // tile] = picked[:, offset : offset + tile]

    def arrive(level, flips):
        z_copy(level, flips).wait_recv()
        for hop in range(1, chips):
            y_copy(level, flips, hop).start()
        c_copy(level, flips, 0).start()

    def relay(level, flips):
        for hop in range(1, chips):
            y_copy(level, flips, hop).wait_recv()
            c_copy(level, flips, hop).start()

    def settle(level):
        def step(flips, carry):
            for hop in range(chips):
                c_copy(level, flips, hop).wait_recv()
            return carry

        lax.fori_loop(1, doms, step, 0)

    group = GROUP

    def initial_group(index):
        span = group * tile
        part = pl.ds(pl.multiple_of(index * span, span), span)
        product = lax.dot_general(
            w_all[...], features[part, :], NT, preferred_element_type=jnp.float32
        )
        product = jnp.maximum(product, 0.0).astype(jnp.bfloat16)
        for offset in range(group):
            initial[index * group + offset] = product[:, offset * tile : (offset + 1) * tile]

    def turn_group(index):
        for offset in range(group):
            row = index * group + offset
            for k in range(per_row):
                values[row, k] = values[row, k].T

    def push(level, buffer):
        return pltpu.make_async_copy(
            buffer.at[:, slice_rows(feat)], pushed_hbm.at[level], out_sem.at[level]
        )

    states = [initial] + [ping if index % 2 == 0 else pong for index in range(layers - 1)]

    def summed(row, first, last, current, halo):
        picked = []
        for k in range(first, last):
            column = columns_ref[k, row]
            if k < OWN_TILES:
                picked.append(current[column])
            else:
                picked.append(halo[jnp.maximum(column - row_tiles, 0)])
        return jnp.dot(
            jnp.concatenate(picked, axis=1),
            values[row, first:last].reshape((last - first) * tile, tile),
            preferred_element_type=jnp.float32,
        )

    def layer_group(layer, index):
        beta = math.log(LAMBDA_DECAY / (layer + 1) + 1.0)
        current, following, halo = states[layer], states[layer + 1], halos[layer]
        first = index * group
        pieces = []
        for offset in range(group):
            row = first + offset
            total = summed(row, 0, per_row, current, halo)
            start = initial[row].astype(jnp.float32)
            pieces.append(((1.0 - ALPHA) * total + ALPHA * start).astype(jnp.bfloat16))
        blended = jnp.concatenate(pieces, axis=1)
        product = jnp.dot(weights_t[layer], blended, preferred_element_type=jnp.float32)
        fresh = jnp.maximum((1.0 - beta) * blended.astype(jnp.float32) + beta * product, 0.0)
        fresh = fresh.astype(jnp.bfloat16)
        for offset in range(group):
            following[first + offset] = fresh[:, offset * tile : (offset + 1) * tile]

    last = layers - 1

    def own_group(index):
        for offset in range(group):
            row = index * group + offset
            total = summed(row, 0, OWN_TILES, states[last], None)
            start = initial[row].astype(jnp.float32)
            partial[row] = (1.0 - ALPHA) * total + ALPHA * start

    def final_copy(index):
        part = pl.ds(index * group, group)
        return pltpu.make_async_copy(final.at[part], final_hbm.at[part], final_sem.at[index])

    def last_group(index):
        beta = math.log(LAMBDA_DECAY / layers + 1.0)
        first = index * group
        pieces = []
        for offset in range(group):
            row = first + offset
            total = summed(row, OWN_TILES, per_row, None, halos[last])
            pieces.append((partial[row] + (1.0 - ALPHA) * total).astype(jnp.bfloat16))
        blended = jnp.concatenate(pieces, axis=1)
        product = jnp.dot(last_w[...], blended, preferred_element_type=jnp.float32)
        fresh = jnp.maximum((1.0 - beta) * product[:width] + beta * product[width:], 0.0)
        fresh = fresh.astype(jnp.bfloat16)
        for offset in range(group):
            final[first + offset] = fresh[:, offset * tile : (offset + 1) * tile]
        final_copy(index).start()

    count = row_tiles // group

    def loop(begin, end, body):
        def step(index, carry):
            body(index)
            return carry

        lax.fori_loop(begin, end, step, 0)

    order = [groups[kind][place] for kind, place in gather_order(doms)]
    loads[0].wait()
    gather(chosen(order, 0))
    pl.semaphore_wait(barrier, doms + feats - 2)
    z_copy(0, chosen(order, 0)).start()
    for step in range(1, feats):
        w_copy(step).start()

    def gather_step(index):
        flips = chosen(order, index)
        gather(flips)
        z_copy(0, flips).start()

    def gather_arrive(index):
        gather_step(index)
        arrive(0, chosen(order, index - GATHER_LAG))

    loop(1, GATHER_LAG, gather_step)
    loop(GATHER_LAG, doms - 1, gather_arrive)
    for level in range(1, layers):
        loop(0, doms - 1, lambda index, level=level: z_copy(level, chosen(order, index)).start())

    for level in range(layers):
        halos[level][block_tiles(dom)] = jnp.zeros((blocks, hidden, tile), jnp.bfloat16)
        weights_t[level] = weights_ref[level].astype(jnp.float32).T.astype(jnp.bfloat16)
    rows_iota = lax.broadcasted_iota(jnp.int32, (width, hidden), 0)
    columns_iota = lax.broadcasted_iota(jnp.int32, (width, hidden), 1)
    last_w[:width] = jnp.where(rows_iota + feat * width == columns_iota, 1.0, 0.0).astype(jnp.bfloat16)
    last_w[width:] = weights_t[last, slice_rows(feat)]
    loop(doms - 1 - GATHER_LAG, doms - 1, lambda index: arrive(0, chosen(order, index)))

    w_all[slice_rows(feat), :] = w_ref[...]
    for step in range(1, feats):
        w_copy(step).wait_recv()
    loads[1].wait()

    works = {
        "initial": initial_group,
        "turn": turn_group,
        "own": own_group,
        "last": last_group,
    }
    for layer in range(last):
        works["layer" + str(layer)] = functools.partial(layer_group, layer)
    done = {name: 0 for name in works}

    def run(name, pieces):
        begin = done[name]
        done[name] = end = min(begin + pieces, count)
        loop(begin, end, works[name])

    def arrivals(code, name=None, each=0):
        table, level = groups[code[0]], int(code[1])
        if name is None or each == 0:
            loop(0, len(table), lambda index: arrive(level, chosen(table, index)))
            return
        begin = done[name]
        fused = min(len(table), (count - begin) // each)
        done[name] = begin + fused * each

        def body(index):
            arrive(level, chosen(table, index))
            for extra in range(each):
                works[name](begin + index * each + extra)

        loop(0, fused, body)
        loop(fused, len(table), lambda index: arrive(level, chosen(table, index)))

    def relays(codes):
        for code in codes.split():
            if code[0] == "A":
                loop(0, doms - 1, lambda index: relay(int(code[1]), chosen(order, index)))
            else:
                table = groups[code[0]]
                loop(0, len(table), lambda index: relay(int(code[1]), chosen(table, index)))

    arrivals("N1", "initial", 2)
    run("initial", count)
    push(0, initial).start()
    loads[2].wait()
    arrivals("O1", "turn", 2)
    run("turn", count)
    relays("A0")
    settle(0)
    for code in ("N2", "N3", "O2"):
        arrivals(code, "layer0", 1)
    run("layer0", count)
    push(1, states[1]).start()
    arrivals("I1")
    relays("N1 O1 I1")
    settle(1)
    arrivals("O3", "layer1", 1)
    run("layer1", count)
    push(2, states[2]).start()
    arrivals("I2")
    relays("N2 O2 I2")
    settle(2)
    push(1, states[1]).wait()
    run("layer2", 4)
    arrivals("I3", "layer2", 1)
    run("layer2", count)
    push(3, states[3]).start()
    run("own", 4)
    relays("N3 O3")
    run("own", count)
    relays("I3")
    settle(3)
    run("last", count)

    for step in range(1, feats):
        w_copy(step).wait_send()
    for level in range(layers):

        def drain(flips, level=level):
            z_copy(level, flips).wait_send()
            for hop in range(chips):
                c_copy(level, flips, hop).wait_send()
            for hop in range(1, chips):
                y_copy(level, flips, hop).wait_send()

        loop(1, doms, drain)
    loop(0, count, lambda index: final_copy(index).wait())
    for level in (0, 2, 3):
        push(level, states[level]).wait()


def on_device(doms, feats, features, w_input, layer_weights, history, tile_values, tile_columns, send_rows, send_counts):
    layers, nodes, width = history.shape
    row_tiles, per_row, tile, _ = tile_values.shape
    cap = send_rows.shape[2]
    hidden = width * feats
    chips = feats // CORES
    any_spec = pl.BlockSpec(memory_space=pl.ANY)
    vmem = pl.BlockSpec(memory_space=pltpu.VMEM)
    smem = pl.BlockSpec(memory_space=pltpu.SMEM)
    bf16 = jnp.bfloat16
    dma = pltpu.SemaphoreType.DMA
    pushed, final = pl.pallas_call(
        functools.partial(kernel, doms, feats, layers, tile),
        out_shape=(
            jax.ShapeDtypeStruct((layers, row_tiles, width, tile), bf16),
            jax.ShapeDtypeStruct((row_tiles, width, tile), bf16),
        ),
        in_specs=[smem, smem, vmem, any_spec, any_spec, vmem, vmem, any_spec],
        out_specs=(any_spec, any_spec),
        scratch_shapes=[pltpu.VMEM((doms * cap // tile, hidden, tile), bf16) for _ in range(layers)] + [
            pltpu.VMEM((layers * width, nodes), bf16),
            pltpu.VMEM(features.shape, bf16),
            pltpu.VMEM((hidden, features.shape[1]), bf16),
            pltpu.VMEM((layers, hidden, hidden), bf16),
            pltpu.VMEM((2 * width, hidden), bf16),
            pltpu.VMEM(tile_values.shape, bf16),
            pltpu.VMEM((doms, cap // tile, layers * width, tile), bf16),
            pltpu.VMEM((row_tiles, hidden, tile), bf16),
            pltpu.VMEM((row_tiles, hidden, tile), bf16),
            pltpu.VMEM((row_tiles, hidden, tile), bf16),
            pltpu.VMEM((row_tiles, hidden, tile), jnp.float32),
            pltpu.VMEM((row_tiles, width, tile), bf16),
            dma((3,)),
            dma((feats,)),
            dma((feats,)),
            dma((layers, doms)),
            dma((layers, doms)),
            dma((layers, doms, chips)),
            dma((layers, doms, chips)),
            dma((layers, doms, chips)),
            dma((layers, doms, chips)),
            dma((layers,)),
            dma((row_tiles // GROUP,)),
        ],
        compiler_params=pltpu.CompilerParams(
            collective_id=0, has_side_effects=True, vmem_limit_bytes=67043328
        ),
    )(
        tile_columns.T,
        send_counts,
        send_rows[0],
        jnp.swapaxes(history, 1, 2).reshape(layers * width, nodes),
        features,
        w_input.T,
        layer_weights,
        tile_values,
    )
    pushed = jnp.transpose(pushed, (0, 1, 3, 2)).reshape(layers, nodes, width)
    return pushed, jnp.transpose(final, (0, 2, 1)).reshape(nodes, width)


def solution(mesh):
    placed = (
        P("dom", None),
        P(None, "feat"),
        P(),
        P(None, "dom", "feat"),
        P("dom", None, None, None),
        P("dom", None),
        P("dom", None, None),
        P("dom", None),
    )
    return jax.shard_map(
        functools.partial(on_device, mesh.shape["dom"], mesh.shape["feat"]),
        mesh=mesh,
        in_specs=placed,
        out_specs=(P(None, "dom", "feat"), P("dom", "feat")),
        check_vma=False,
    )
```

time: 79.8 us -> 88.2 us (1.11)
  Pallas kernels: 74.8 us -> 82.4 us
    pallas_call x1, Pallas kernels: 74.8 us -> 82.4 us  [on_device(): pl.pallas_call(functools.partial(kernel, doms, feats, layers, tile), out_...]
where the time goes in v1:
time: 88.2 us; the launch traced here: 87.2 us
  Pallas kernels  82.4 us (93%)
  local copies, waits for them, and re-layouts  4.16 us (5%)
    pallas_call x1, Pallas kernels, on_device(): pl.pallas_call(functools.partial(kernel, doms, feats, layers, tile), out_...  82.4 us
    reshape x1, local copies, waits for them, and re-layouts, on_device(): pushed = jnp.transpose(pushed, (0, 1, 3, 2)).reshape(layers, nodes, width)  3.29 us

profile of v1, /device:TPU:0, one launch (start us, length us, event | category | flops | bytes accessed | tf_op | source)
XLA Modules:
  0.0 87.2 jit_solution(16197337032380927859)
XLA Ops:
  0.6 82.4 %shard_map.95 = (bf16[4,32,64,128]{3,2,1,0:T(8,128)(2,1)}, bf16[32,64,128]{2,1,0:T(8,128)(2,1)}) custom-call(s32[6,32]{1,0:T(8,128)} %bitcast.21, s32[1,8]{1,0:T(1,128)} %counts_ref.1, s32[8,512]{1,0:T(8,128)} %bitcast.19, bf16[256,4096]{1,0:T(8,128)(2,1)} %bitcast.18, bf16[4096,128]{1,0:T(8,128)(2,1)} %features_hbm.1, bf16[64,128]{1,0:T(8,128)(2,1)} %bitcast.20, ...), custom_call_target="tpu_custom_call" | custom-call | tf_op jit(solution)/shard_map/pallas_call | solution.py:406
  83.0 0.0 copy-start
  83.0 3.3 %copy_bitcast_fusion = bf16[4,4096,64]{1,2,0:T(8,128)(2,1)} fusion(bf16[4,32,64,128]{3,2,1,0:T(8,128)(2,1)} %get-tuple-element.4), kind=kLoop, calls=%fused_computation | loop fusion | bytes 4194304 | tf_op jit(solution)/shard_map/reshape | solution.py:452
  86.3 0.0 copy-done
  86.3 0.9 copy_bitcast_fusion.1
Async XLA Ops:
  83.0 3.3 %copy-start = (bf16[32,64,128]{2,1,0:T(8,128)(2,1)S(1)}, bf16[32,64,128]{2,1,0:T(8,128)(2,1)}, u32[]{:S(2)}) copy-start(bf16[32,64,128]{2,1,0:T(8,128)(2,1)} %get-tuple-element.5) | copy-start | bytes 1572868

commit v2 on v1

v2 whole, which is shorter than its diff:
```python
import functools
import math

import jax
import jax.numpy as jnp
from jax import lax
from jax.experimental import pallas as pl
from jax.experimental.pallas import tpu as pltpu
from jax.sharding import PartitionSpec as P

ALPHA = 0.1
LAMBDA_DECAY = 0.5
CORES = 2
GROUP = 8
ORDER = ("O0", "I0", "O1", "I1", "X0", "N0", "N1")
ARRIVALS = (
    ("G0", "H0", "N0", "X0", "N1", "N2", "O1", "X1", "I1")
    + ("N3", "X2", "O2", "I2", "X3", "O3", "I3")
)
EARLY = 6
LAG = 4
PACE_KIND = "O"
SLACK = 1
OWN_TILES = 2
MESH = pl.DeviceIdType.MESH
NT = (((1,), (1,)), ((), ()))


def kernel(
    doms, feats, layers, tile, columns_ref, counts_ref, rows_hbm, history_hbm, features_hbm,
    w_hbm, weights_hbm, values_hbm, pushed_ref, final_ref, *scratch
):
    halos = scratch[:layers]
    (rows_ref, w_ref, weights_ref, history, features, w_all, weights_t, last_w, values, outgoing, initial, ping, pong, partial,
     load_sem, w_send, w_recv, z_send, z_recv, y_send, y_recv, c_send, c_recv) = scratch[layers:]
    width = w_ref.shape[0]
    nodes = history.shape[1]
    cap = rows_ref.shape[1]
    row_tiles, per_row = values.shape[0], values.shape[1]
    hidden = width * feats
    chips = feats // CORES
    dom = lax.axis_index("dom")
    feat = lax.axis_index("feat")
    chip, core = feat // CORES, feat % CORES
    sibling = chip * CORES + (1 - core)

    half, quarter = doms // 2, doms // 4
    inside = lax.rem(dom // quarter + 1, 4) // 2
    near = [(flips, 0) for flips in range(2, half)]
    outer = [(half + quarter + index, -quarter) for index in range(quarter)]
    inner = [(half + index, quarter) for index in range(quarter)]
    groups = {"X": [(1, 0)], "N": near, "O": outer, "I": inner}

    def chosen(table, index):
        if isinstance(index, int):
            base, slope = table[index]
            return base + slope * inside
        value = 0
        for place, (base, slope) in enumerate(table):
            value = value + jnp.where(index == place, base + slope * inside, 0)
        return value

    def partner(flips):
        dest, bit = dom, 1
        while bit < doms:
            dest = dest + lax.rem(flips // bit, 2) * (bit - 2 * bit * lax.rem(dom // bit, 2))
            bit *= 2
        return dest

    barrier = pltpu.get_barrier_semaphore()
    for step in range(1, doms):
        pl.semaphore_signal(
            barrier, inc=1, device_id={"dom": lax.rem(dom + step, doms)}, device_id_type=MESH
        )
    for step in range(1, feats):
        pl.semaphore_signal(
            barrier, inc=1, device_id={"feat": lax.rem(feat + step, feats)}, device_id_type=MESH
        )
    for hop in range(1, chips):
        across = {"dom": partner(1), "feat": lax.rem(chip + hop, chips) * CORES + core}
        pl.semaphore_signal(barrier, inc=1, device_id=across, device_id_type=MESH)

    rows_load = pltpu.make_async_copy(rows_hbm, rows_ref, load_sem.at[5])
    loads = [
        pltpu.make_async_copy(history_hbm, history, load_sem.at[0]),
        pltpu.make_async_copy(features_hbm, features, load_sem.at[1]),
        pltpu.make_async_copy(values_hbm, values, load_sem.at[2]),
        pltpu.make_async_copy(w_hbm, w_ref, load_sem.at[3]),
        pltpu.make_async_copy(weights_hbm, weights_ref, load_sem.at[4]),
    ]
    for load in (loads[0], rows_load, *loads[1:]):
        load.start()

    def slice_rows(index):
        return pl.ds(pl.multiple_of(index * width, width), width)

    blocks = cap // tile

    def block_tiles(source):
        return pl.ds(source * blocks, blocks)

    def w_copy(step):
        return pltpu.make_async_remote_copy(
            src_ref=w_ref,
            dst_ref=w_all.at[slice_rows(feat)],
            send_sem=w_send.at[step],
            recv_sem=w_recv.at[step],
            device_id={"feat": lax.rem(feat + step, feats)},
            device_id_type=MESH,
        )

    def z_copy(level, flips):
        return pltpu.make_async_remote_copy(
            src_ref=outgoing.at[flips, :, pl.ds(level * width, width)],
            dst_ref=halos[level].at[block_tiles(dom), slice_rows(feat)],
            send_sem=z_send.at[0],
            recv_sem=z_recv.at[level, flips],
            device_id={"dom": partner(flips)},
            device_id_type=MESH,
        )

    def y_copy(level, flips, hop):
        block = halos[level].at[block_tiles(partner(flips)), slice_rows(feat)]
        return pltpu.make_async_remote_copy(
            src_ref=block,
            dst_ref=block,
            send_sem=y_send.at[hop],
            recv_sem=y_recv.at[level, flips, hop],
            device_id={"feat": lax.rem(chip + hop, chips) * CORES + core},
            device_id_type=MESH,
        )

    def x_copy(level, hop):
        return pltpu.make_async_remote_copy(
            src_ref=outgoing.at[1, :, pl.ds(level * width, width)],
            dst_ref=halos[level].at[block_tiles(dom), slice_rows(feat)],
            send_sem=y_send.at[hop],
            recv_sem=y_recv.at[level, 1, hop],
            device_id={"dom": partner(1), "feat": lax.rem(chip + hop, chips) * CORES + core},
            device_id_type=MESH,
        )

    def x_send(level):
        z_copy(level, 1).start()
        for hop in range(1, chips):
            x_copy(level, hop).start()

    def c_copy(level, flips, hop):
        owner = lax.rem(chip + chips - hop, chips) * CORES + core
        block = halos[level].at[block_tiles(partner(flips)), slice_rows(owner)]
        return pltpu.make_async_remote_copy(
            src_ref=block,
            dst_ref=block,
            send_sem=c_send.at[hop],
            recv_sem=c_recv.at[level],
            device_id={"feat": sibling},
            device_id_type=MESH,
        )

    def gather(flips):
        dest = partner(flips)
        part = min(cap, 256)
        for begin in range(0, cap, part):
            slots = begin + lax.broadcasted_iota(jnp.int32, (1, part), 1)
            rows = rows_ref[pl.ds(dest, 1), pl.ds(begin, part)]
            rows = jnp.where(slots < counts_ref[0, dest], rows, -1)
            nodes_iota = lax.broadcasted_iota(jnp.int32, (nodes, part), 0)
            onehot = jnp.where(nodes_iota == rows, 1.0, 0.0).astype(jnp.bfloat16)
            picked = jnp.dot(history[...], onehot, preferred_element_type=jnp.float32)
            picked = picked.astype(jnp.bfloat16)
            for offset in range(0, part, tile):
                outgoing[flips, (begin + offset) // tile] = picked[:, offset : offset + tile]

    def arrive(level, kind, flips, index):
        z_copy(level, flips).wait_recv()
        if kind == "N" and level + 2 < layers:
            z_copy(level + 2, flips).start()
        if kind == PACE_KIND and level + 1 < layers:

            @pl.when(inside == 0)
            def _():
                z_copy(level + 1, chosen(outer, index)).start()
                z_copy(level + 1, chosen(inner, index)).start()

        if kind != "X":
            for hop in range(1, chips):
                y_copy(level, flips, hop).start()
        elif level + 2 < layers:
            x_send(level + 2)
        c_copy(level, flips, 0).start()

    def relay(level, flips):
        for hop in range(1, chips):
            y_copy(level, flips, hop).wait_recv()
            c_copy(level, flips, hop).start()

    def settle(level):
        span = halos[level].at[pl.ds(0, (doms - 1) * chips * blocks // feats)]
        pltpu.make_async_remote_copy(
            src_ref=span,
            dst_ref=span,
            send_sem=c_send.at[0],
            recv_sem=c_recv.at[level],
            device_id={"feat": sibling},
            device_id_type=MESH,
        ).wait_recv()

    def drain(sem):
        span = outgoing.at[pl.ds(1, doms - 1)]
        pltpu.make_async_remote_copy(
            src_ref=span,
            dst_ref=span,
            send_sem=sem,
            recv_sem=c_recv.at[0],
            device_id={"feat": sibling},
            device_id_type=MESH,
        ).wait_send()

    group = GROUP

    def initial_group(index):
        span = group * tile
        part = pl.ds(pl.multiple_of(index * span, span), span)
        product = lax.dot_general(
            w_all[...], features[part, :], NT, preferred_element_type=jnp.float32
        )
        product = jnp.maximum(product, 0.0).astype(jnp.bfloat16)
        for offset in range(group):
            initial[index * group + offset] = product[:, offset * tile : (offset + 1) * tile]

    states = [initial] + [ping if index % 2 == 0 else pong for index in range(layers - 1)]

    def summed(row, first, last, current, halo):
        picked = []
        for k in range(first, last):
            column = columns_ref[k, row]
            if k < OWN_TILES:
                picked.append(current[column])
            else:
                picked.append(halo[jnp.maximum(column - row_tiles, 0)])
        return lax.dot_general(
            jnp.concatenate(picked, axis=1),
            jnp.concatenate([values[row, k] for k in range(first, last)], axis=1),
            NT,
            preferred_element_type=jnp.float32,
        )

    last = layers - 1

    def own_group(layer, index):
        for offset in range(group):
            row = index * group + offset
            total = summed(row, 0, OWN_TILES, states[layer], None)
            start = initial[row].astype(jnp.float32)
            partial[row] = (1.0 - ALPHA) * total + ALPHA * start
            columns = pl.ds(pl.multiple_of(row * tile, tile), tile)
            pushed_ref[layer, :, columns] = states[layer][row, slice_rows(feat), :]

    def blended_group(layer, index):
        pieces = []
        for offset in range(group):
            row = index * group + offset
            total = summed(row, OWN_TILES, per_row, None, halos[layer])
            pieces.append((partial[row] + (1.0 - ALPHA) * total).astype(jnp.bfloat16))
        return jnp.concatenate(pieces, axis=1)

    def layer_group(layer, index):
        beta = math.log(LAMBDA_DECAY / (layer + 1) + 1.0)
        following = states[layer + 1]
        blended = blended_group(layer, index)
        product = jnp.dot(weights_t[layer], blended, preferred_element_type=jnp.float32)
        fresh = jnp.maximum((1.0 - beta) * blended.astype(jnp.float32) + beta * product, 0.0)
        fresh = fresh.astype(jnp.bfloat16)
        for offset in range(group):
            following[index * group + offset] = fresh[:, offset * tile : (offset + 1) * tile]

    def last_group(index):
        beta = math.log(LAMBDA_DECAY / layers + 1.0)
        blended = blended_group(last, index)
        product = jnp.dot(last_w[...], blended, preferred_element_type=jnp.float32)
        fresh = jnp.maximum((1.0 - beta) * product[:width] + beta * product[width:], 0.0)
        fresh = fresh.astype(jnp.bfloat16)
        span = group * tile
        final_ref[:, pl.ds(pl.multiple_of(index * span, span), span)] = fresh

    count = row_tiles // group

    def loop(begin, end, body):
        def step(index, carry):
            body(index)
            return carry

        lax.fori_loop(begin, end, step, 0)

    order = [groups[code[0]][int(code[1:])] for code in ORDER]
    rows_load.wait()
    loads[0].wait()
    gather(chosen(order, 0))
    pl.semaphore_wait(barrier, doms + feats + chips - 3)
    if order[0] == (1, 0):
        x_send(0)
        x_send(1)
    else:
        z_copy(0, chosen(order, 0)).start()
    loads[3].wait()
    for step in range(1, feats):
        w_copy(step).start()

    def gather_step(index):
        flips = chosen(order, index)
        gather(flips)
        z_copy(0, flips).start()

    far = [entry for pair in zip(outer, inner) for entry in pair]
    arriving = []
    for code in ARRIVALS:
        level = int(code[1])
        if code[0] in "GH":
            part = far[: half // 2] if code[0] == "G" else far[half // 2 :]
            arriving += [(level, entry, "O" if entry in outer else "I") for entry in part]
        else:
            arriving += [(level, entry, code[0]) for entry in groups[code[0]]]
    early = doms - 1 - EARLY

    cross = order.index((1, 0))

    def gather_span(begin, end):
        if begin <= cross < end:
            loop(begin, cross, gather_step)
            gather(1)
            x_send(0)
            x_send(1)
            begin = cross + 1
        loop(begin, end, gather_step)

    gather_span(1, EARLY)
    for index in range(early):
        gather_span(EARLY + index, EARLY + index + 1)
        level, entry, kind = arriving[index]
        arrive(level, kind, chosen([entry], 0), groups[kind].index(entry))
    loop(0, len(near), lambda index: z_copy(1, chosen(near, index)).start())

    @pl.when(inside == 1)
    def _():
        for level in range(1, layers):
            loop(0, quarter, lambda index: z_copy(level, chosen(outer, index)).start())
            loop(0, quarter, lambda index: z_copy(level, chosen(inner, index)).start())

    loads[4].wait()
    for level in range(layers):
        halos[level][block_tiles(dom)] = jnp.zeros((blocks, hidden, tile), jnp.bfloat16)
        weights_t[level] = weights_ref[level].astype(jnp.float32).T.astype(jnp.bfloat16)
    rows_iota = lax.broadcasted_iota(jnp.int32, (width, hidden), 0)
    columns_iota = lax.broadcasted_iota(jnp.int32, (width, hidden), 1)
    last_w[:width] = jnp.where(rows_iota + feat * width == columns_iota, 1.0, 0.0).astype(jnp.bfloat16)
    last_w[width:] = weights_t[last, slice_rows(feat)]

    w_all[slice_rows(feat), :] = w_ref[...]
    for step in range(1, feats):
        w_copy(step).wait_recv()
    loads[1].wait()

    works = {"initial": initial_group}
    for layer in range(last):
        works["own" + str(layer)] = functools.partial(own_group, layer)
        works["layer" + str(layer)] = functools.partial(layer_group, layer)
    works["own" + str(last)] = functools.partial(own_group, last)
    works["last"] = last_group
    done = {name: 0 for name in works}

    def run(name, pieces):
        begin = done[name]
        done[name] = end = min(begin + pieces, count)
        loop(begin, end, works[name])

    final_step = len(arriving) + LAG
    covered = [
        max(place for place, entry in enumerate(arriving) if entry[0] == layer) + LAG + 1
        for layer in range(layers)
    ]

    def before(name):
        if name == "own0":
            loads[2].wait()
        if name.startswith("layer"):
            settle(int(name[5:]))
        if name == "last":
            settle(last)

    pieces = [("initial", 0)] * count
    for layer in range(last):
        pieces += [("own" + str(layer), 0)] * count
        pieces += [("layer" + str(layer), covered[layer] + SLACK)] * count
    pieces += [("own" + str(last), 0)] * count
    plan = []
    for step in range(early, final_step):
        piece = pieces.pop(0)[0] if pieces and pieces[0][1] <= step else None
        plan.append(
            (
                arriving[step] if step < len(arriving) else None,
                arriving[step - LAG] if step >= LAG else None,
                piece,
            )
        )

    def like(entry):
        arrived, relayed, piece = entry
        return (arrived and (arrived[0], arrived[2]), relayed and relayed[0], piece)

    while plan:
        length = 1
        while length < len(plan) and like(plan[length]) == like(plan[0]):
            length += 1
        part, plan = plan[:length], plan[length:]
        arrived, relayed, piece = part[0]
        begin = 0
        if piece:
            begin = done[piece]
            done[piece] += length
            if begin == 0:
                before(piece)

        def body(index, part=part, arrived=arrived, relayed=relayed, piece=piece, begin=begin):
            if arrived:
                table = [entry[0][1] for entry in part]
                place = groups[arrived[2]].index(table[0]) + index
                arrive(arrived[0], arrived[2], chosen(table, index), place)
            if relayed:
                relay(relayed[0], chosen([entry[1][1] for entry in part], index))
            if piece:
                works[piece](begin + index)

        loop(0, length, body)
    for name in [*works]:
        if done[name] < count:
            if done[name] == 0:
                before(name)
            run(name, count)

    for step in range(1, feats):
        w_copy(step).wait_send()
    drain(z_send.at[0])
    for hop in range(1, chips):
        drain(y_send.at[hop])
    for hop in range(chips):
        drain(c_send.at[hop])


def on_device(doms, feats, features, w_input, layer_weights, history, tile_values, tile_columns, send_rows, send_counts):
    layers, nodes, width = history.shape
    row_tiles, per_row, tile, _ = tile_values.shape
    cap = send_rows.shape[2]
    hidden = width * feats
    chips = feats // CORES
    any_spec = pl.BlockSpec(memory_space=pl.ANY)
    smem = pl.BlockSpec(memory_space=pltpu.SMEM)
    bf16 = jnp.bfloat16
    dma = pltpu.SemaphoreType.DMA
    pushed, final = pl.pallas_call(
        functools.partial(kernel, doms, feats, layers, tile),
        out_shape=(
            pltpu.VMEM((layers, width, nodes), bf16),
            pltpu.VMEM((width, nodes), bf16),
        ),
        in_specs=[smem, smem] + [any_spec] * 6,
        out_specs=(pl.BlockSpec(memory_space=pltpu.VMEM), pl.BlockSpec(memory_space=pltpu.VMEM)),
        scratch_shapes=[pltpu.VMEM((doms * cap // tile, hidden, tile), bf16) for _ in range(layers)] + [
            pltpu.VMEM(send_rows.shape[1:], jnp.int32),
            pltpu.VMEM((width, features.shape[1]), bf16),
            pltpu.VMEM(layer_weights.shape, bf16),
            pltpu.VMEM((layers * width, nodes), bf16),
            pltpu.VMEM(features.shape, bf16),
            pltpu.VMEM((hidden, features.shape[1]), bf16),
            pltpu.VMEM((layers, hidden, hidden), bf16),
            pltpu.VMEM((2 * width, hidden), bf16),
            pltpu.VMEM(tile_values.shape, bf16),
            pltpu.VMEM((doms, cap // tile, layers * width, tile), bf16),
            pltpu.VMEM((row_tiles, hidden, tile), bf16),
            pltpu.VMEM((row_tiles, hidden, tile), bf16),
            pltpu.VMEM((row_tiles, hidden, tile), bf16),
            pltpu.VMEM((row_tiles, hidden, tile), jnp.float32),
            dma((6,)),
            dma((feats,)),
            dma((feats,)),
            dma((1,)),
            dma((layers, doms)),
            dma((chips,)),
            dma((layers, doms, chips)),
            dma((chips,)),
            dma((layers,)),
        ],
        compiler_params=pltpu.CompilerParams(
            collective_id=0, has_side_effects=True, vmem_limit_bytes=67043328 - 2 * (layers + 1) * width * nodes
        ),
    )(
        tile_columns.T,
        send_counts,
        send_rows[0],
        jnp.swapaxes(history, 1, 2).reshape(layers * width, nodes),
        features,
        w_input.T,
        layer_weights,
        tile_values,
    )
    return jnp.swapaxes(pushed, 1, 2), final.T


def solution(mesh):
    placed = (
        P("dom", None),
        P(None, "feat"),
        P(),
        P(None, "dom", "feat"),
        P("dom", None, None, None),
        P("dom", None),
        P("dom", None, None),
        P("dom", None),
    )
    return jax.shard_map(
        functools.partial(on_device, mesh.shape["dom"], mesh.shape["feat"]),
        mesh=mesh,
        in_specs=placed,
        out_specs=(P(None, "dom", "feat"), P("dom", "feat")),
        check_vma=False,
    )
```

time: 88.2 us -> 67.9 us (0.77)
  Pallas kernels: 82.4 us -> 64.9 us
  local copies, waits for them, and re-layouts: 4.16 us -> 2.11 us
    pallas_call x1, Pallas kernels: 82.4 us -> 64.9 us  [on_device(): pl.pallas_call(functools.partial(kernel, doms, feats, layers, tile), out_...]
    reshape x2 -> x0, local copies, waits for them, and re-layouts: 4.16 us -> none  [the longest x1 3.29 us: on_device(): pushed = jnp.transpose(pushed, (0, 1, 3, 2)).reshape(layers, nodes, width)]
    unnamed x2, local copies, waits for them, and re-layouts: 0.01 us -> 2.11 us
where the time goes in v2:
time: 67.9 us; the launch traced here: 67.7 us
  Pallas kernels  64.9 us (96%)
  local copies, waits for them, and re-layouts  2.11 us (3%)
    pallas_call x1, Pallas kernels, on_device(): pl.pallas_call(functools.partial(kernel, doms, feats, layers, tile), out_...  64.9 us
    unnamed x2, local copies, waits for them, and re-layouts  2.11 us

profile of v2, /device:TPU:0, one launch (start us, length us, event | category | flops | bytes accessed | tf_op | source)
XLA Modules:
  0.0 67.7 jit_solution(6902904186329381789)
XLA Ops:
  0.6 64.9 %shard_map.95 = (bf16[4,64,4096]{2,1,0:T(8,128)(2,1)S(1)}, bf16[64,4096]{1,0:T(8,128)(2,1)S(1)}) custom-call(s32[6,32]{1,0:T(8,128)} %bitcast.13, s32[1,8]{1,0:T(1,128)} %counts_ref.1, s32[8,512]{1,0:T(8,128)} %bitcast.11, bf16[256,4096]{1,0:T(8,128)(2,1)} %bitcast.10, bf16[4096,128]{1,0:T(8,128)(2,1)} %features_hbm.1, bf16[64,128]{1,0:T(8,128)(2,1)} %bitcast.12, ...), custom_call_target="tpu_custom_call" | custom-call | tf_op jit(solution)/shard_map/pallas_call | solution.py:459
  65.6 1.3 %copy.12 = bf16[4,4096,64]{1,2,0:T(8,128)(2,1)} copy(bf16[4,4096,64]{1,2,0:T(8,128)(2,1)S(1)} %bitcast.8) | data formatting | bytes 4194304
  66.9 0.8 %copy.13 = bf16[4096,64]{0,1:T(8,128)(2,1)} copy(bf16[4096,64]{0,1:T(8,128)(2,1)S(1)} %bitcast.9) | data formatting | bytes 1048576

commit v3 on v2

--- a/solution.py
+++ b/solution.py
@@ -18,9 +18,10 @@
     + ("N3", "X2", "O2", "I2", "X3", "O3", "I3")
 )
 EARLY = 6
-LAG = 4
-PACE_KIND = "O"
-SLACK = 1
+LAG = 5
+PACE_KINDS = ("O", "O", "O")
+WIDE = 2
+SLACK = 0
 OWN_TILES = 2
 MESH = pl.DeviceIdType.MESH
 NT = (((1,), (1,)), ((), ()))
@@ -175,7 +176,7 @@
         z_copy(level, flips).wait_recv()
         if kind == "N" and level + 2 < layers:
             z_copy(level + 2, flips).start()
-        if kind == PACE_KIND and level + 1 < layers:
+        if level + 1 < layers and kind == PACE_KINDS[level]:
 
             @pl.when(inside == 0)
             def _():
@@ -256,7 +257,7 @@
             columns = pl.ds(pl.multiple_of(row * tile, tile), tile)
             pushed_ref[layer, :, columns] = states[layer][row, slice_rows(feat), :]
 
-    def blended_group(layer, index):
+    def blended_group(layer, index, group=group):
         pieces = []
         for offset in range(group):
             row = index * group + offset
@@ -276,11 +277,11 @@
 
     def last_group(index):
         beta = math.log(LAMBDA_DECAY / layers + 1.0)
-        blended = blended_group(last, index)
+        blended = blended_group(last, index, WIDE * group)
         product = jnp.dot(last_w[...], blended, preferred_element_type=jnp.float32)
         fresh = jnp.maximum((1.0 - beta) * product[:width] + beta * product[width:], 0.0)
         fresh = fresh.astype(jnp.bfloat16)
-        span = group * tile
+        span = WIDE * group * tile
         final_ref[:, pl.ds(pl.multiple_of(index * span, span), span)] = fresh
 
     count = row_tiles // group
@@ -371,6 +372,8 @@
     def run(name, pieces):
         begin = done[name]
         done[name] = end = min(begin + pieces, count)
+        if name == "last":
+            end //= WIDE
         loop(begin, end, works[name])
 
     final_step = len(arriving) + LAG

time: 67.9 us -> 65.9 us (0.971)
  Pallas kernels: 64.9 us -> 62.6 us
    pallas_call x1, Pallas kernels: 64.9 us -> 62.6 us  [on_device(): pl.pallas_call(functools.partial(kernel, doms, feats, layers, tile), out_...]
where the time goes in v3:
time: 65.9 us; the launch traced here: 65.4 us
  Pallas kernels  62.6 us (95%)
  local copies, waits for them, and re-layouts  2.11 us (3%)
    pallas_call x1, Pallas kernels, on_device(): pl.pallas_call(functools.partial(kernel, doms, feats, layers, tile), out_...  62.6 us
    unnamed x2, local copies, waits for them, and re-layouts  2.11 us

profile of v3, /device:TPU:0, one launch (start us, length us, event | category | flops | bytes accessed | tf_op | source)
XLA Modules:
  0.0 65.4 jit_solution(3519773833242541658)
XLA Ops:
  0.6 62.6 %shard_map.95 = (bf16[4,64,4096]{2,1,0:T(8,128)(2,1)S(1)}, bf16[64,4096]{1,0:T(8,128)(2,1)S(1)}) custom-call(s32[6,32]{1,0:T(8,128)} %bitcast.13, s32[1,8]{1,0:T(1,128)} %counts_ref.1, s32[8,512]{1,0:T(8,128)} %bitcast.11, bf16[256,4096]{1,0:T(8,128)(2,1)} %bitcast.10, bf16[4096,128]{1,0:T(8,128)(2,1)} %features_hbm.1, bf16[64,128]{1,0:T(8,128)(2,1)} %bitcast.12, ...), custom_call_target="tpu_custom_call" | custom-call | tf_op jit(solution)/shard_map/pallas_call | solution.py:462
  63.3 1.3 %copy.12 = bf16[4,4096,64]{1,2,0:T(8,128)(2,1)} copy(bf16[4,4096,64]{1,2,0:T(8,128)(2,1)S(1)} %bitcast.8) | data formatting | bytes 4194304
  64.6 0.8 %copy.13 = bf16[4096,64]{0,1:T(8,128)(2,1)} copy(bf16[4096,64]{0,1:T(8,128)(2,1)S(1)} %bitcast.9) | data formatting | bytes 1048576
